TPU v7x, 32 devices: a whole 2x2x4 slice. The times are simulated.
32 devices in a mesh: grp: 2 (over y), seq: 8 (over z, x), tp: 2 (over core).
Axes of the slice: x: 2, y: 2, z: 4, core: 2. Of those that a mesh axis runs over, the one named last changes fastest.
Arguments:
- queries: bfloat16 [4096, 2048], P(('grp', 'seq'), 'tp'), parts along dimension 0, may hold values from -9 to 9
- keys: bfloat16 [4096, 2048], P(('grp', 'seq'), 'tp'), parts along dimension 0, may hold values from -9 to 9
- values: bfloat16 [4096, 2048], P(('grp', 'seq'), 'tp'), parts along dimension 0, may hold values from -18 to 18
- segment_ids: int32 [4096], P(('grp', 'seq')), parts along dimension 0, may hold values from 0 to 7, never falling along the last dimension, each value on 1 to 512 neighbouring positions
- modality: int32 [4096], P(('grp', 'seq')), parts along dimension 0, may hold values 0 or 1
- norm_gain: float32 [2, 2048], P(None, 'tp'), may hold values from 0.1 to 1.9
Outputs:
- blended: bfloat16 [4096, 2048], P(('grp', 'seq'), 'tp'), parts along dimension 0
There are 2 independent parts, one for each index of `grp`. A program takes and returns all parts, laid end to end along the dimension named above; an argument that names none is the same for every part. Nothing has to cross between parts.
Inputs may be any that keep to these rules, and one draw needn't show every extreme that they name: `segment_ids`: ids never fall along the sequence; each document holds 1 to 512 tokens, and one holds exactly that many.
All inputs are finite; a program needn't handle non-finite values. No bound on the sum of `modality` on one device may be relied on, other than what follows from the above.
Results may differ from a plain program's by a relative error of at most 0.009.
Values may be sent and summed in bfloat16 or wider, within the bound.
A program may use at most 64 MiB of HBM per device.

v0:
```python
import jax
import jax.numpy as jnp
from jax import lax
from jax.sharding import PartitionSpec as P

HEADS = 16
HEAD_DIM = 128
REACH = 2


def shifted(value, axis, steps):
    count = lax.axis_size(axis)
    initial, last = (max(0, -steps), min(count, count - steps))
    return lax.ppermute(value, axis, [(source, source + steps) for source in range(initial, last)])


def on_device(queries, keys, values, segment_ids, modality, norm_gain):
    tok_rows, feat_width = queries.shape
    head_count = feat_width // HEAD_DIM
    my_index = lax.axis_index("seq")
    score_scale = HEAD_DIM ** (-0.5)
    query_heads = queries.reshape(tok_rows, head_count, HEAD_DIM)
    offsets = jnp.arange(tok_rows, dtype=jnp.int32)
    query_pos = my_index * tok_rows + offsets

    def absorb(running, key_block, value_block, key_segs, distance):
        run_max, run_total, run_acc = running
        scores = (
            jnp.einsum(
                "qhd,khd->hqk",
                query_heads,
                key_block.reshape(tok_rows, head_count, HEAD_DIM),
                preferred_element_type=jnp.float32,
            )
            * score_scale
        )
        key_pos = (my_index - distance) * tok_rows + offsets
        allowed = (
            (segment_ids[:, None] == key_segs[None, :])
            & (key_pos[None, :] <= query_pos[:, None])
            & (my_index >= distance)
        )
        scores = jnp.where(allowed[None], scores, -jnp.inf)
        new_max = jnp.maximum(run_max, jnp.max(scores, axis=2))
        weights = jnp.exp(scores - new_max[:, :, None])
        factor = jnp.exp(run_max - new_max)
        new_total = run_total * factor + jnp.sum(weights, axis=2)
        contrib = jnp.einsum(
            "hqk,khd->hqd",
            weights.astype(jnp.bfloat16),
            value_block.reshape(tok_rows, head_count, HEAD_DIM),
            preferred_element_type=jnp.float32,
        )
        return (new_max, new_total, run_acc * factor[:, :, None] + contrib)

    start_state = (
        jnp.full((head_count, tok_rows), -jnp.inf, jnp.float32),
        jnp.zeros((head_count, tok_rows), jnp.float32),
        jnp.zeros((head_count, tok_rows, HEAD_DIM), jnp.float32),
    )
    running = absorb(start_state, keys, values, segment_ids, 0)
    for distance in range(1, REACH + 1):
        arrived = shifted((keys, values, segment_ids), "seq", distance)
        running = absorb(running, arrived[0], arrived[1], arrived[2], distance)
    run_max, run_total, run_acc = running
    attended = (run_acc / run_total[:, :, None]).astype(jnp.bfloat16)
    attended = jnp.transpose(attended, (1, 0, 2)).reshape(tok_rows, feat_width).astype(jnp.float32)
    partial_value = jnp.sum(attended * attended, axis=1)
    total = lax.psum(partial_value, "tp")
    mean_square = total / (HEADS * HEAD_DIM)
    gain_rows = jnp.where((modality == 1)[:, None], norm_gain[1][None, :], norm_gain[0][None, :])
    blended = attended * lax.rsqrt(mean_square + 1e-05)[:, None] * gain_rows
    return blended.astype(jnp.bfloat16)


def solution(mesh):
    return jax.shard_map(
        on_device,
        mesh=mesh,
        in_specs=(
            P(("grp", "seq"), "tp"),
            P(("grp", "seq"), "tp"),
            P(("grp", "seq"), "tp"),
            P(("grp", "seq")),
            P(("grp", "seq")),
            P(None, "tp"),
        ),
        out_specs=P(("grp", "seq"), "tp"),
        check_vma=False,
    )
```

profile of v0, /device:TPU:11, one launch (start us, length us, event | category | flops | bytes accessed | tf_op | source)
XLA Modules:
  0.0 65.1 jit_solution(13082774962858657751)
XLA Ops:
  0.0 0.0 copy-start
  0.0 0.0 copy-start.4
  0.0 0.0 copy-start.3
  0.0 3.3 %collective-permute-start = (s32[256]{0:T(256)}, s32[256]{0:T(256)S(1)}, u32[]{:S(2)}, u32[]{:S(2)}) collective-permute-start(s32[256]{0:T(256)} %param.9), channel_id=1, source_target_pairs={{0,2},{2,4},{4,6},{6,8},{8,10},{10,12},{12,14},{1,3},{3,5},{5,7},{... | collective-permute-start | bytes 3080 | tf_op jit(solution)/shard_map/ppermute | solution.py:14
  3.3 3.2 %collective-permute-start.3 = (s32[256]{0:T(256)}, s32[256]{0:T(256)S(1)}, u32[]{:S(2)}, u32[]{:S(2)}) collective-permute-start(s32[256]{0:T(256)} %param.9), channel_id=1, source_target_pairs={{0,4},{2,6},{4,8},{6,10},{8,12},{10,14},{1,5},{3,7},{5,9},{7,11},{... | collective-permute-start | bytes 3080 | tf_op jit(solution)/shard_map/ppermute | solution.py:14
  6.5 1.2 %copy.22 = bf16[256,1024]{0,1:T(8,128)(2,1)S(1)} copy(bf16[256,1024]{1,0:T(8,128)(2,1)} %param.7) | data formatting | bytes 1048576 | tf_op args[1]
  7.8 1.9 %collective-permute-start.4 = (bf16[256,1024]{0,1:T(8,128)(2,1)S(1)}, bf16[256,1024]{0,1:T(8,128)(2,1)S(1)}, u32[]{:S(2)}, u32[]{:S(2)}) collective-permute-start(bf16[256,1024]{0,1:T(8,128)(2,1)S(1)} %copy.22), channel_id=1, source_target_pairs={{0,4},{2,6},{4,8},{6,10},{8,12},{10,14},{1,5},{3,7},{5,9},{7,11},{... | collective-permute-start | bytes 1572872 | tf_op jit(solution)/shard_map/ppermute | solution.py:14
  9.7 3.1 %collective-permute-start.1 = (bf16[256,1024]{0,1:T(8,128)(2,1)S(1)}, bf16[256,1024]{0,1:T(8,128)(2,1)S(1)}, u32[]{:S(2)}, u32[]{:S(2)}) collective-permute-start(bf16[256,1024]{0,1:T(8,128)(2,1)S(1)} %copy.22), channel_id=1, source_target_pairs={{0,2},{2,4},{4,6},{6,8},{8,10},{10,12},{12,14},{1,3},{3,5},{5,7},{... | collective-permute-start | bytes 1572872 | tf_op jit(solution)/shard_map/ppermute | solution.py:14
  12.8 1.9 %collective-permute-start.2 = (bf16[256,1024]{1,0:T(8,128)(2,1)}, bf16[256,1024]{1,0:T(8,128)(2,1)}, u32[]{:S(2)}, u32[]{:S(2)}) collective-permute-start(bf16[256,1024]{1,0:T(8,128)(2,1)} %param.8), channel_id=1, source_target_pairs={{0,2},{2,4},{4,6},{6,8},{8,10},{10,12},{12,14},{1,3},{3,5},{5,7},{... | collective-permute-start | bytes 1572872 | tf_op jit(solution)/shard_map/ppermute | solution.py:14
  14.8 0.8 %fusion.58 = (f32[1,1024]{1,0:T(1,128)S(1)}, f32[1,1024]{1,0:T(1,128)S(1)}) fusion(f32[2,1024]{1,0:T(2,128)} %param.11), kind=kLoop, calls=%fused_computation.79 | loop fusion | bytes 16384 | tf_op jit(solution)/shard_map/slice | solution.py:71
  15.6 0.7 %broadcast_compare_fusion = pred[256]{0:T(512)(128)(4,1)S(1)} fusion(s32[256]{0:T(256)} %param.10), kind=kLoop, calls=%fused_computation.71 | loop fusion | flops 256 | bytes 1280 | tf_op jit(solution)/shard_map/eq | solution.py:71
  16.3 2.0 %copy.38 = bf16[256,1024]{0,1:T(8,128)(2,1)} copy(bf16[256,1024]{1,0:T(8,128)(2,1)} %param.8) | data formatting | bytes 1048576 | tf_op jit(solution)/shard_map/reshape | solution.py:51
  18.3 0.0 collective-permute-done
  18.3 1.9 %collective-permute-start.5 = (bf16[256,1024]{1,0:T(8,128)(2,1)}, bf16[256,1024]{1,0:T(8,128)(2,1)}, u32[]{:S(2)}, u32[]{:S(2)}) collective-permute-start(bf16[256,1024]{1,0:T(8,128)(2,1)} %param.8), channel_id=1, source_target_pairs={{0,4},{2,6},{4,8},{6,10},{8,12},{10,14},{1,5},{3,7},{5,9},{7,11},{... | collective-permute-start | bytes 1572872 | tf_op jit(solution)/shard_map/ppermute | solution.py:14
  20.2 0.0 collective-permute-done.3
  20.3 0.0 copy-done.4
  20.3 0.3 and_and_fusion.1
  20.6 0.0 copy-done
  20.6 0.0 copy-done.3
  20.6 0.5 fusion
  21.1 0.0 copy-start.2
  21.1 0.9 %collective-permute-done.4 = bf16[256,1024]{0,1:T(8,128)(2,1)S(1)} collective-permute-done((bf16[256,1024]{0,1:T(8,128)(2,1)S(1)}, bf16[256,1024]{0,1:T(8,128)(2,1)S(1)}, u32[]{:S(2)}, u32[]{:S(2)}) %collective-permute-start.4) | collective-permute-done | bytes 524320 | tf_op jit(solution)/shard_map/ppermute | solution.py:14
  21.9 0.5 fusion.2
  22.5 0.0 copy-start.1
  22.5 8.8 %collective-permute-done.1 = bf16[256,1024]{0,1:T(8,128)(2,1)S(1)} collective-permute-done((bf16[256,1024]{0,1:T(8,128)(2,1)S(1)}, bf16[256,1024]{0,1:T(8,128)(2,1)S(1)}, u32[]{:S(2)}, u32[]{:S(2)}) %collective-permute-start.1) | collective-permute-done | bytes 524320 | tf_op jit(solution)/shard_map/ppermute | solution.py:14
  31.3 0.6 fusion.1
  31.8 0.0 copy-done.2
  31.8 0.9 %fusion.3 = (f32[8,256]{1,0:T(8,128)S(1)}, f32[8,256]{1,0:T(8,128)S(1)}) fusion(f32[8,256,256]{1,2,0:T(8,128)S(1)} %get-tuple-element.17, f32[8,256]{1,0:T(8,128)S(1)} %get-tuple-element.16, pred[256,256]{0,1:T(8,128)(4,1)S(1)} %get-tuple-element.15, f32[8,256]{1,0:T(8,128)S(1)} %get-tuple-element.9, f32[8,256,256]{1,2,0:T(8,128)S(1)} %get-tuple-element.21, ...), kind=kLoop, calls=%fused_computation.9 | loop fusion | flops 4190208 | bytes 4358144 | tf_op jit(solution)/shard_map/reduce_sum | solution.py:47
  32.7 0.0 copy-done.1
  32.8 0.4 fusion.7
  33.2 9.4 %collective-permute-done.2 = bf16[256,1024]{1,0:T(8,128)(2,1)} collective-permute-done((bf16[256,1024]{1,0:T(8,128)(2,1)}, bf16[256,1024]{1,0:T(8,128)(2,1)}, u32[]{:S(2)}, u32[]{:S(2)}) %collective-permute-start.2) | collective-permute-done | bytes 524320 | tf_op jit(solution)/shard_map/ppermute | solution.py:14
  42.6 1.2 %copy.25 = bf16[256,1024]{0,1:T(8,128)(2,1)S(1)} copy(bf16[256,1024]{1,0:T(8,128)(2,1)} %collective-permute-done.2) | data formatting | bytes 1048576 | tf_op jit(solution)/shard_map/ppermute | solution.py:14
  43.8 2.4 %fusion.14 = f32[256,8,128]{0,2,1:T(8,128)S(1)} fusion(bf16[256,8,128]{0,2,1:T(8,128)(2,1)} %bitcast.114, f32[8,256,256]{1,2,0:T(8,128)} %copy-done.2, f32[8,256]{1,0:T(8,128)S(1)} %get-tuple-element.16, pred[256,256]{0,1:T(8,128)(4,1)S(1)} %get-tuple-element.15, f32[256,8]{0,1:T(8,128)S(1)} %get-tuple-element.7, f32[256,8]{0,1:T(8,128)S(1)} %get-tuple-element.12), kind=kOutput, calls=%fused_computation.23 | convolution fusion | flops 136839168 | bytes 3760128 | tf_op jit(solution)/shard_map/hqk,khd->hqd/dot_general | solution.py:48
  46.3 1.7 %fusion.12 = f32[256,8,128]{0,2,1:T(8,128)} fusion(f32[256,8,128]{0,2,1:T(8,128)S(1)} %fusion.14, bf16[256,8,128]{0,2,1:T(8,128)(2,1)S(1)} %bitcast.110, f32[8,256,256]{1,2,0:T(8,128)S(1)} %get-tuple-element.21, f32[8,256]{1,0:T(8,128)S(1)} %get-tuple-element.9, pred[256,256]{0,1:T(8,128)(4,1)S(1)} %get-tuple-element.13, f32[256,8]{0,1:T(8,128)S(1)} %get-tuple-element.6), kind=kOutput, calls=%fused_computation.20 | convolution fusion | flops 136839168 | bytes 4800512 | tf_op jit(solution)/shard_map/hqk,khd->hqd/dot_general | solution.py:48
  47.9 7.8 %collective-permute-done.5 = bf16[256,1024]{1,0:T(8,128)(2,1)} collective-permute-done((bf16[256,1024]{1,0:T(8,128)(2,1)}, bf16[256,1024]{1,0:T(8,128)(2,1)}, u32[]{:S(2)}, u32[]{:S(2)}) %collective-permute-start.5) | collective-permute-done | bytes 524320 | tf_op jit(solution)/shard_map/ppermute | solution.py:14
  55.7 1.2 %copy.30 = bf16[256,1024]{0,1:T(8,128)(2,1)S(1)} copy(bf16[256,1024]{1,0:T(8,128)(2,1)} %collective-permute-done.5) | data formatting | bytes 1048576 | tf_op jit(solution)/shard_map/ppermute | solution.py:14
  57.0 2.5 %multiply_reduce_fusion = (f32[256]{0:T(256)S(1)}, f32[256,8,128]{0,2,1:T(8,128)S(1)}) fusion(f32[256,8]{0,1:T(8,128)S(1)} %get-tuple-element.5, f32[256,8,128]{0,2,1:T(8,128)} %fusion.12, bf16[256,8,128]{0,2,1:T(8,128)(2,1)S(1)} %bitcast.115, f32[8,256,256]{1,2,0:T(8,128)} %copy-done.1, f32[8,256]{1,0:T(8,128)S(1)} %get-tuple-element.8, ...), kind=kOutput, calls=%fused_computation.27 | convolution fusion | flops 137887488 | bytes 4801536 | tf_op jit(solution)/shard_map/hqk,khd->hqd/dot_general | solution.py:48
  59.5 0.3 copy.32
  59.8 4.2 %psum.7 = f32[256]{0:T(256)S(1)} all-reduce(f32[256]{0:T(256)S(1)} %get-tuple-element.22), channel_id=1, replica_groups=mesh['grp'=2,'seq'=8,'tp'=2] {'tp'}, use_global_device_ids=true, to_apply=%region_7.8 | all-reduce | flops 256 | bytes 2048 | tf_op jit(solution)/shard_map/psum | solution.py:69
  64.1 1.0 %multiply_convert_fusion = bf16[256,1024]{1,0:T(8,128)(2,1)} fusion(f32[256,1024]{1,0:T(8,128)S(1)} %copy.32, f32[1024]{0:T(1024)S(1)} %bitcast.117, f32[1024]{0:T(1024)S(1)} %bitcast.116, f32[256]{0:T(256)S(1)} %add_rsqrt_fusion, pred[256]{0:T(512)(128)(4,1)S(1)} %broadcast_compare_fusion), kind=kLoop, calls=%fused_computation.26 | loop fusion | flops 1048576 | bytes 1582336 | tf_op jit(solution)/shard_map/convert_element_type | solution.py:73
  (6 shorter events, 0.0 us)
Async XLA Ops:
  0.0 20.6 %copy-start = (bf16[256,1024]{1,0:T(8,128)(2,1)S(1)}, bf16[256,1024]{1,0:T(8,128)(2,1)}, u32[]{:S(2)}) copy-start(bf16[256,1024]{1,0:T(8,128)(2,1)} %param.6) | copy-start | bytes 1572868
  0.0 20.3 %copy-start.4 = (s32[256]{0:T(256)S(1)}, s32[256]{0:T(256)}, u32[]{:S(2)}) copy-start(s32[256]{0:T(256)} %param.9) | copy-start | bytes 3076
  0.0 20.6 %copy-start.3 = (bf16[256,1024]{1,0:T(8,128)(2,1)S(1)}, bf16[256,1024]{1,0:T(8,128)(2,1)}, u32[]{:S(2)}) copy-start(bf16[256,1024]{1,0:T(8,128)(2,1)} %param.7) | copy-start | bytes 1572868
  0.0 18.3 %collective-permute-start = (s32[256]{0:T(256)}, s32[256]{0:T(256)S(1)}, u32[]{:S(2)}, u32[]{:S(2)}) collective-permute-start(s32[256]{0:T(256)} %param.9), channel_id=1, source_target_pairs={{0,2},{2,4},{4,6},{6,8},{8,10},{10,12},{12,14},{1,3},{3,5},{5,7},{... | collective-permute-start | bytes 3080 | tf_op jit(solution)/shard_map/ppermute | solution.py:14
  3.3 16.9 %collective-permute-start.3 = (s32[256]{0:T(256)}, s32[256]{0:T(256)S(1)}, u32[]{:S(2)}, u32[]{:S(2)}) collective-permute-start(s32[256]{0:T(256)} %param.9), channel_id=1, source_target_pairs={{0,4},{2,6},{4,8},{6,10},{8,12},{10,14},{1,5},{3,7},{5,9},{7,11},{... | collective-permute-start | bytes 3080 | tf_op jit(solution)/shard_map/ppermute | solution.py:14
  7.8 14.1 %collective-permute-start.4 = (bf16[256,1024]{0,1:T(8,128)(2,1)S(1)}, bf16[256,1024]{0,1:T(8,128)(2,1)S(1)}, u32[]{:S(2)}, u32[]{:S(2)}) collective-permute-start(bf16[256,1024]{0,1:T(8,128)(2,1)S(1)} %copy.22), channel_id=1, source_target_pairs={{0,4},{2,6},{4,8},{6,10},{8,12},{10,14},{1,5},{3,7},{5,9},{7,11},{... | collective-permute-start | bytes 1572872 | tf_op jit(solution)/shard_map/ppermute | solution.py:14
  9.7 21.5 %collective-permute-start.1 = (bf16[256,1024]{0,1:T(8,128)(2,1)S(1)}, bf16[256,1024]{0,1:T(8,128)(2,1)S(1)}, u32[]{:S(2)}, u32[]{:S(2)}) collective-permute-start(bf16[256,1024]{0,1:T(8,128)(2,1)S(1)} %copy.22), channel_id=1, source_target_pairs={{0,2},{2,4},{4,6},{6,8},{8,10},{10,12},{12,14},{1,3},{3,5},{5,7},{... | collective-permute-start | bytes 1572872 | tf_op jit(solution)/shard_map/ppermute | solution.py:14
  12.8 29.8 %collective-permute-start.2 = (bf16[256,1024]{1,0:T(8,128)(2,1)}, bf16[256,1024]{1,0:T(8,128)(2,1)}, u32[]{:S(2)}, u32[]{:S(2)}) collective-permute-start(bf16[256,1024]{1,0:T(8,128)(2,1)} %param.8), channel_id=1, source_target_pairs={{0,2},{2,4},{4,6},{6,8},{8,10},{10,12},{12,14},{1,3},{3,5},{5,7},{... | collective-permute-start | bytes 1572872 | tf_op jit(solution)/shard_map/ppermute | solution.py:14
  18.3 37.4 %collective-permute-start.5 = (bf16[256,1024]{1,0:T(8,128)(2,1)}, bf16[256,1024]{1,0:T(8,128)(2,1)}, u32[]{:S(2)}, u32[]{:S(2)}) collective-permute-start(bf16[256,1024]{1,0:T(8,128)(2,1)} %param.8), channel_id=1, source_target_pairs={{0,4},{2,6},{4,8},{6,10},{8,12},{10,14},{1,5},{3,7},{5,9},{7,11},{... | collective-permute-start | bytes 1572872 | tf_op jit(solution)/shard_map/ppermute | solution.py:14
  21.1 10.8 %copy-start.2 = (f32[8,256,256]{1,2,0:T(8,128)}, f32[8,256,256]{1,2,0:T(8,128)S(1)}, u32[]{:S(2)}) copy-start(f32[8,256,256]{1,2,0:T(8,128)S(1)} %get-tuple-element.17) | copy-start | bytes 6291460
  22.5 10.3 %copy-start.1 = (f32[8,256,256]{1,2,0:T(8,128)}, f32[8,256,256]{1,2,0:T(8,128)S(1)}, u32[]{:S(2)}) copy-start(f32[8,256,256]{1,2,0:T(8,128)S(1)} %get-tuple-element.19) | copy-start | bytes 6291460
where the time goes:
time: 65.6 us; the launch traced here: 65.1 us
  waiting for transfers between devices  26.8 us (41%)
  starting transfers between devices  15.4 us (23%)
  matrix products  8.17 us (12%)
  local copies, waits for them, and re-layouts  6.9 us (11%)
  blocking collectives  4.22 us (6%)
  other arithmetic  3.36 us (5%)
    ppermute x6, waiting for transfers between devices, shifted(): lax.ppermute(value, axis, [(source, source + steps) for source in range(i...  26.8 us
    ppermute x6, starting transfers between devices, shifted(): lax.ppermute(value, axis, [(source, source + steps) for source in range(i...  15.4 us
    dot_general x3, matrix products, absorb(): jnp.einsum('hqk,khd->hqd', weights.astype(jnp.bfloat16), value_block.resh...  6.6 us
    psum x1, blocking collectives, on_device(): total = lax.psum(partial_value, 'tp')  4.22 us
    ppermute x2, local copies, waits for them, and re-layouts, shifted(): lax.ppermute(value, axis, [(source, source + steps) for source in range(i...  2.49 us
    reshape x1, local copies, waits for them, and re-layouts, absorb(): value_block.reshape(tok_rows, head_count, HEAD_DIM)  2.04 us
    dot_general x3, matrix products, absorb(): jnp.einsum('qhd,khd->hqk', query_heads, key_block.reshape(tok_rows, head_...  1.57 us
    reduce_sum x2, other arithmetic, absorb(): new_total = run_total * factor + jnp.sum(weights, axis=2)  1.36 us
  transfers between devices with their start and end apart: 6, of which 4 were waited for; matrix products, arithmetic and copies ran while one was open for 20% of the time, Pallas kernels for 0%

commit v1 on v0

v1 whole, which is shorter than its diff:
```python
import functools

import jax
import jax.numpy as jnp
from jax import lax
from jax.experimental import pallas as pl
from jax.experimental.pallas import tpu as pltpu
from jax.sharding import PartitionSpec as P

HEADS = 16
HEAD_DIM = 128
REACH = 2
MESH = pl.DeviceIdType.MESH


def kernel(
    n,
    heads,
    rows,
    q_hbm,
    k_hbm,
    v_hbm,
    seg_ref,
    mod_ref,
    gain_ref,
    out_ref,
    q_own,
    own,
    buf1,
    buf2,
    seg1,
    seg2,
    bias,
    att,
    squares,
    mine,
    theirs,
    in_sem,
    send_a,
    send_b,
    send_c,
    recv_1,
    recv_2,
    seg_send,
    seg_recv,
    sq_sem,
):
    s = lax.axis_index("seq")
    t = lax.axis_index("tp")
    even = lax.rem(s, 2) == 0
    odd = lax.rem(s, 2) == 1
    has_next = s + 2 < n
    has_prev = s >= 2
    pair = s + 1 - 2 * lax.rem(s, 2)

    def load(source, target, h, j):
        columns = pl.ds(h * HEAD_DIM, HEAD_DIM)
        return pltpu.make_async_copy(source.at[:, columns], target, in_sem.at[h, j])

    def load_k(h):
        return load(k_hbm, own.at[h, 0], h, 0)

    def load_v(h):
        return load(v_hbm, own.at[h, 1], h, 1)

    def load_q(h):
        return load(q_hbm, q_own.at[h], h, 2)

    for h in range(heads):
        load_k(h).start()
        load_v(h).start()

    barrier = pltpu.get_barrier_semaphore()
    pl.semaphore_signal(barrier, inc=1, device_id={"tp": 1 - t}, device_id_type=MESH)
    pl.semaphore_signal(barrier, inc=1, device_id={"seq": pair}, device_id_type=MESH)

    @pl.when(has_next)
    def _():
        pl.semaphore_signal(barrier, inc=1, device_id={"seq": s + 2}, device_id_type=MESH)

    @pl.when(has_prev)
    def _():
        pl.semaphore_signal(barrier, inc=1, device_id={"seq": s - 2}, device_id_type=MESH)

    peers = 2 + jnp.where(has_next, 1, 0) + jnp.where(has_prev, 1, 0)
    pl.semaphore_wait(barrier, peers)

    def remote(source, target, send, recv, where):
        return pltpu.make_async_remote_copy(
            src_ref=source,
            dst_ref=target,
            send_sem=send,
            recv_sem=recv,
            device_id={"seq": where},
            device_id_type=MESH,
        )

    def flow_a(h):
        return remote(own.at[h], buf1.at[h], send_a.at[h], recv_1.at[h], pair)

    def flow_b(h):
        return remote(own.at[h], buf2.at[h], send_b.at[h], recv_2.at[h], s + 2)

    def flow_c(h):
        return remote(buf2.at[h], buf1.at[h], send_c.at[h], recv_1.at[h], pair)

    def seg_a():
        return remote(seg_ref, seg1, seg_send.at[0], seg_recv.at[0], pair)

    def seg_b():
        return remote(seg_ref, seg2, seg_send.at[1], seg_recv.at[1], s + 2)

    def seg_c():
        return remote(seg2, seg1, seg_send.at[2], seg_recv.at[0], pair)

    @pl.when(even)
    def _():
        seg_a().start()

    @pl.when(has_next)
    def _():
        seg_b().start()

    def send(h, carry):
        load_k(h).wait()
        load_v(h).wait()

        @pl.when(has_next)
        def _():
            flow_b(h).start()

        @pl.when(even)
        def _():
            flow_a(h).start()

        load_q(h).start()
        return carry

    lax.fori_loop(0, heads, send, 0)

    @pl.when(s < 1)
    def _():
        buf1[...] = jnp.zeros_like(buf1)
        seg1[...] = jnp.full_like(seg1, -1)

    @pl.when(s < 2)
    def _():
        buf2[...] = jnp.zeros_like(buf2)
        seg2[...] = jnp.full_like(seg2, -1)

    def column(row):
        return jnp.transpose(jnp.broadcast_to(row, (HEAD_DIM, rows)))

    query_seg = column(seg_ref[...])[:, :1]
    query_pos = lax.broadcasted_iota(jnp.int32, (rows, rows), 0)
    key_pos = lax.broadcasted_iota(jnp.int32, (rows, rows), 1)
    allowed = (query_seg == seg_ref[...]) & (key_pos <= query_pos)
    bias[:, :rows] = jnp.where(allowed, 0.0, -jnp.inf)
    squares[...] = jnp.zeros_like(squares)

    @pl.when(has_prev)
    def _():
        seg_b().wait_recv()

    @pl.when(odd & has_prev)
    def _():
        seg_c().start()

    @pl.when(s >= 1)
    def _():
        seg_a().wait_recv()

    bias[:, rows : 2 * rows] = jnp.where(query_seg == seg1[...], 0.0, -jnp.inf)
    bias[:, 2 * rows :] = jnp.where(query_seg == seg2[...], 0.0, -jnp.inf)

    def scores_of(query, key):
        return lax.dot_general(
            query, key, (((1,), (1,)), ((), ())), preferred_element_type=jnp.float32
        )

    def head(h, carry):
        load_q(h).wait()

        @pl.when(has_prev)
        def _():
            flow_b(h).wait_recv()

        @pl.when(odd & has_prev)
        def _():
            flow_c(h).start()

        @pl.when(s >= 1)
        def _():
            flow_a(h).wait_recv()

        query = q_own[h]
        scale = HEAD_DIM ** (-0.5)
        blocks = (own, buf1, buf2)
        scores = [
            scores_of(query, block[h, 0]) * scale + bias[:, i * rows : (i + 1) * rows]
            for i, block in enumerate(blocks)
        ]
        top = jnp.maximum(jnp.maximum(scores[0], scores[1]), scores[2])
        top = jnp.max(top, axis=1, keepdims=True)
        weights = [jnp.exp(score - top) for score in scores]
        total = jnp.sum(weights[0] + weights[1] + weights[2], axis=1, keepdims=True)
        acc = jnp.zeros((rows, HEAD_DIM), jnp.float32)
        for weight, block in zip(weights, blocks):
            acc = acc + jnp.dot(
                weight.astype(jnp.bfloat16), block[h, 1], preferred_element_type=jnp.float32
            )
        attended = (acc * (1.0 / total)).astype(jnp.bfloat16)
        att[h] = attended
        wide = attended.astype(jnp.float32)
        squares[...] += wide * wide
        return carry

    lax.fori_loop(0, heads, head, 0)

    partial = jnp.sum(squares[...], axis=1, keepdims=True)
    mine[...] = jnp.broadcast_to(partial, mine.shape)
    swap = pltpu.make_async_remote_copy(
        src_ref=mine,
        dst_ref=theirs,
        send_sem=sq_sem.at[0],
        recv_sem=sq_sem.at[1],
        device_id={"tp": 1 - t},
        device_id_type=MESH,
    )
    swap.start()
    image = column(mod_ref[...]) == 1
    swap.wait_recv()
    mean_square = (mine[...] + theirs[...]) / (HEADS * HEAD_DIM)
    inverse = lax.rsqrt(mean_square + 1e-05)
    for h in range(heads):
        columns = slice(h * HEAD_DIM, (h + 1) * HEAD_DIM)
        gain = jnp.where(image, gain_ref[1:2, columns], gain_ref[0:1, columns])
        out_ref[:, columns] = (att[h].astype(jnp.float32) * inverse * gain).astype(out_ref.dtype)

    swap.wait_send()

    @pl.when(even)
    def _():
        seg_a().wait_send()

    @pl.when(has_next)
    def _():
        seg_b().wait_send()

    @pl.when(odd & has_prev)
    def _():
        seg_c().wait_send()

    def drain(h, carry):
        @pl.when(even)
        def _():
            flow_a(h).wait_send()

        @pl.when(has_next)
        def _():
            flow_b(h).wait_send()

        @pl.when(odd & has_prev)
        def _():
            flow_c(h).wait_send()

        return carry

    lax.fori_loop(0, heads, drain, 0)


def on_device(n, queries, keys, values, segment_ids, modality, norm_gain):
    rows, width = queries.shape
    heads = width // HEAD_DIM
    vmem = pl.BlockSpec(memory_space=pltpu.VMEM)
    hbm = pl.BlockSpec(memory_space=pl.ANY)
    block = pltpu.VMEM((heads, 2, rows, HEAD_DIM), jnp.bfloat16)
    return pl.pallas_call(
        functools.partial(kernel, n, heads, rows),
        out_shape=jax.ShapeDtypeStruct((rows, width), jnp.bfloat16),
        in_specs=[hbm, hbm, hbm, vmem, vmem, vmem],
        out_specs=vmem,
        scratch_shapes=[
            pltpu.VMEM((heads, rows, HEAD_DIM), jnp.bfloat16),
            block,
            block,
            block,
            pltpu.VMEM((1, rows), jnp.int32),
            pltpu.VMEM((1, rows), jnp.int32),
            pltpu.VMEM((rows, (REACH + 1) * rows), jnp.float32),
            pltpu.VMEM((heads, rows, HEAD_DIM), jnp.bfloat16),
            pltpu.VMEM((rows, HEAD_DIM), jnp.float32),
            pltpu.VMEM((rows, HEAD_DIM), jnp.float32),
            pltpu.VMEM((rows, HEAD_DIM), jnp.float32),
            pltpu.SemaphoreType.DMA((heads, 3)),
            pltpu.SemaphoreType.DMA((heads,)),
            pltpu.SemaphoreType.DMA((heads,)),
            pltpu.SemaphoreType.DMA((heads,)),
            pltpu.SemaphoreType.DMA((heads,)),
            pltpu.SemaphoreType.DMA((heads,)),
            pltpu.SemaphoreType.DMA((3,)),
            pltpu.SemaphoreType.DMA((2,)),
            pltpu.SemaphoreType.DMA((2,)),
        ],
        compiler_params=pltpu.CompilerParams(collective_id=0, has_side_effects=True),
    )(
        queries,
        keys,
        values,
        segment_ids.reshape(1, rows),
        modality.reshape(1, rows),
        norm_gain,
    )


def solution(mesh):
    return jax.shard_map(
        functools.partial(on_device, mesh.shape["seq"]),
        mesh=mesh,
        in_specs=(
            P(("grp", "seq"), "tp"),
            P(("grp", "seq"), "tp"),
            P(("grp", "seq"), "tp"),
            P(("grp", "seq")),
            P(("grp", "seq")),
            P(None, "tp"),
        ),
        out_specs=P(("grp", "seq"), "tp"),
        check_vma=False,
    )
```

time: 65.6 us -> 37.3 us (0.57)
  the two profiles are of different devices: /device:TPU:11 before, /device:TPU:17 now
where the time goes in v1:
time: 37.3 us; the launch traced here: 37 us
  Pallas kernels  35.2 us (94%)
  local copies, waits for them, and re-layouts  1.87 us (5%)
    pallas_call x1, Pallas kernels, on_device(): pl.pallas_call(functools.partial(kernel, n, heads, rows), out_shape=jax.S...  35.2 us
    unnamed x1, local copies, waits for them, and re-layouts  1.87 us

profile of v1, /device:TPU:17, one launch (start us, length us, event | category | flops | bytes accessed | tf_op | source)
XLA Modules:
  0.0 37.0 jit_solution(7077373264090267629)
XLA Ops:
  0.0 35.2 %shard_map.64 = bf16[256,1024]{1,0:T(8,128)(2,1)} custom-call(bf16[256,1024]{1,0:T(8,128)(2,1)} %q_hbm.1, bf16[256,1024]{1,0:T(8,128)(2,1)} %k_hbm.1, bf16[256,1024]{1,0:T(8,128)(2,1)} %v_hbm.1, s32[1,256]{1,0:T(1,128)} %bitcast.2, s32[1,256]{1,0:T(1,128)} %bitcast.3, f32[2,1024]{1,0:T(2,128)} %gain_ref.1), custom_call_target="tpu_custom_call" | custom-call | tf_op jit(solution)/shard_map/pallas_call | solution.py:278
  35.2 1.9 %copy.8 = bf16[256,1024]{1,0:T(8,128)(2,1)} copy(bf16[256,1024]{1,0:T(8,128)(2,1)} %shard_map.64) | data formatting | bytes 1048576

commit v2 on v1

v2 whole, which is shorter than its diff:
```python
import functools

import jax
import jax.numpy as jnp
from jax import lax
from jax.experimental import pallas as pl
from jax.experimental.pallas import tpu as pltpu
from jax.sharding import PartitionSpec as P

HEADS = 16
HEAD_DIM = 128
REACH = 2
MESH = pl.DeviceIdType.MESH
PIECES = 4


def kernel(
    n,
    heads,
    rows,
    q_hbm,
    k_hbm,
    v_hbm,
    seg_ref,
    mod_ref,
    att,
    inverse_ref,
    image_ref,
    q_own,
    own,
    buf1,
    buf2,
    seg1,
    seg2,
    bias,
    squares,
    mine,
    theirs,
    in_sem,
    send_a,
    send_b,
    send_c,
    recv_1,
    recv_2,
    seg_send,
    seg_recv,
    sq_sem,
):
    s = lax.axis_index("seq")
    t = lax.axis_index("tp")
    even = lax.rem(s, 2) == 0
    odd = lax.rem(s, 2) == 1
    has_next = s + 2 < n
    has_prev = s >= 2
    pair = s + 1 - 2 * lax.rem(s, 2)

    half = PIECES // 2
    depth = rows // half

    def columns_of(h):
        return pl.ds(h * HEAD_DIM, HEAD_DIM)

    def load_piece(h, p):
        source = k_hbm if p < half else v_hbm
        piece = pl.ds((p % half) * depth, depth)
        return pltpu.make_async_copy(
            source.at[piece, columns_of(h)], own.at[h, p], in_sem.at[h, p]
        )

    def load_q(h):
        return pltpu.make_async_copy(q_hbm.at[:, columns_of(h)], q_own.at[h], in_sem.at[h, PIECES])

    for h in range(heads):
        for p in range(PIECES):
            load_piece(h, p).start()

    barrier = pltpu.get_barrier_semaphore()
    pl.semaphore_signal(barrier, inc=1, device_id={"tp": 1 - t}, device_id_type=MESH)
    pl.semaphore_signal(barrier, inc=1, device_id={"seq": pair}, device_id_type=MESH)

    @pl.when(has_next)
    def _():
        pl.semaphore_signal(barrier, inc=1, device_id={"seq": s + 2}, device_id_type=MESH)

    @pl.when(has_prev)
    def _():
        pl.semaphore_signal(barrier, inc=1, device_id={"seq": s - 2}, device_id_type=MESH)

    peers = 2 + jnp.where(has_next, 1, 0) + jnp.where(has_prev, 1, 0)
    pl.semaphore_wait(barrier, peers)

    def remote(source, target, send, recv, where):
        return pltpu.make_async_remote_copy(
            src_ref=source,
            dst_ref=target,
            send_sem=send,
            recv_sem=recv,
            device_id={"seq": where},
            device_id_type=MESH,
        )

    def flow_a(h, p):
        return remote(own.at[h, p], buf1.at[h, p], send_a.at[h, p], recv_1.at[h, p], pair)

    def flow_b(h, p):
        return remote(own.at[h, p], buf2.at[h, p], send_b.at[h, p], recv_2.at[h, p], s + 2)

    def flow_c(h, p):
        return remote(buf2.at[h, p], buf1.at[h, p], send_c.at[h, p], recv_1.at[h, p], pair)

    def seg_a():
        return remote(seg_ref, seg1, seg_send.at[0], seg_recv.at[0], pair)

    def seg_b():
        return remote(seg_ref, seg2, seg_send.at[1], seg_recv.at[1], s + 2)

    def seg_c():
        return remote(seg2, seg1, seg_send.at[2], seg_recv.at[0], pair)

    @pl.when(even)
    def _():
        seg_a().start()

    @pl.when(has_next)
    def _():
        seg_b().start()

    def send(h, carry):
        for p in range(PIECES):
            load_piece(h, p).wait()

            @pl.when(has_next)
            def _():
                flow_b(h, p).start()

            @pl.when(even)
            def _():
                flow_a(h, p).start()

        load_q(h).start()
        return carry

    lax.fori_loop(0, heads, send, 0)

    @pl.when(s < 1)
    def _():
        buf1[...] = jnp.zeros_like(buf1)
        seg1[...] = jnp.full_like(seg1, -1)

    @pl.when(s < 2)
    def _():
        buf2[...] = jnp.zeros_like(buf2)
        seg2[...] = jnp.full_like(seg2, -1)

    def column(row):
        return jnp.transpose(jnp.broadcast_to(row, (HEAD_DIM, rows)))

    query_seg = column(seg_ref[...])[:, :1]
    query_pos = lax.broadcasted_iota(jnp.int32, (rows, rows), 0)
    key_pos = lax.broadcasted_iota(jnp.int32, (rows, rows), 1)
    allowed = (query_seg == seg_ref[...]) & (key_pos <= query_pos)
    bias[:, :rows] = jnp.where(allowed, 0.0, -jnp.inf)
    squares[...] = jnp.zeros_like(squares)
    image_ref[...] = column(mod_ref[...])

    @pl.when(has_prev)
    def _():
        seg_b().wait_recv()

    @pl.when(odd & has_prev)
    def _():
        seg_c().start()

    @pl.when(s >= 1)
    def _():
        seg_a().wait_recv()

    bias[:, rows : 2 * rows] = jnp.where(query_seg == seg1[...], 0.0, -jnp.inf)
    bias[:, 2 * rows :] = jnp.where(query_seg == seg2[...], 0.0, -jnp.inf)

    def scores_of(query, key):
        return lax.dot_general(
            query, key, (((1,), (1,)), ((), ())), preferred_element_type=jnp.float32
        )

    def arrive(h, pieces):
        for p in pieces:

            @pl.when(s >= 1)
            def _():
                flow_a(h, p).wait_recv()

    def head(h, carry):
        load_q(h).wait()
        query = q_own[h]
        scale = HEAD_DIM ** (-0.5)

        def scores_with(block, i):
            key = block[h, :half].reshape(rows, HEAD_DIM)
            return scores_of(query, key) * scale + bias[:, i * rows : (i + 1) * rows]

        def product(weight, block):
            value = block[h, half:].reshape(rows, HEAD_DIM)
            return jnp.dot(
                weight.astype(jnp.bfloat16), value, preferred_element_type=jnp.float32
            )

        for p in range(PIECES):

            @pl.when(has_prev)
            def _():
                flow_b(h, p).wait_recv()

            @pl.when(odd & has_prev)
            def _():
                flow_c(h, p).start()

        near = scores_with(own, 0)
        far = scores_with(buf2, 2)
        arrive(h, range(half))
        middle = scores_with(buf1, 1)
        top = jnp.max(jnp.maximum(jnp.maximum(near, middle), far), axis=1, keepdims=True)
        near = jnp.exp(near - top)
        far = jnp.exp(far - top)
        middle = jnp.exp(middle - top)
        total = jnp.sum(near + middle + far, axis=1, keepdims=True)
        acc = product(near, own) + product(far, buf2)
        arrive(h, range(half, PIECES))
        acc = acc + product(middle, buf1)
        attended = (acc * (1.0 / total)).astype(jnp.bfloat16)
        att[h] = attended
        wide = attended.astype(jnp.float32)
        squares[...] += wide * wide
        return carry

    lax.fori_loop(0, heads, head, 0)

    partial = jnp.sum(squares[...], axis=1, keepdims=True)
    mine[...] = jnp.broadcast_to(partial, mine.shape)
    swap = pltpu.make_async_remote_copy(
        src_ref=mine,
        dst_ref=theirs,
        send_sem=sq_sem.at[0],
        recv_sem=sq_sem.at[1],
        device_id={"tp": 1 - t},
        device_id_type=MESH,
    )
    swap.start()
    swap.wait_recv()
    mean_square = (mine[...] + theirs[...]) / (HEADS * HEAD_DIM)
    inverse_ref[...] = lax.rsqrt(mean_square + 1e-05)
    swap.wait_send()

    @pl.when(even)
    def _():
        seg_a().wait_send()

    @pl.when(has_next)
    def _():
        seg_b().wait_send()

    @pl.when(odd & has_prev)
    def _():
        seg_c().wait_send()

    def drain(h, carry):
        for p in range(PIECES):

            @pl.when(even)
            def _():
                flow_a(h, p).wait_send()

            @pl.when(has_next)
            def _():
                flow_b(h, p).wait_send()

            @pl.when(odd & has_prev)
            def _():
                flow_c(h, p).wait_send()

        return carry

    lax.fori_loop(0, heads, drain, 0)


def blend(heads, att, inverse_ref, image_ref, gain_ref, out_hbm, staged, out_sem):
    inverse = inverse_ref[...]
    image = image_ref[...] == 1
    copies = []
    for h in range(heads):
        columns = slice(h * HEAD_DIM, (h + 1) * HEAD_DIM)
        gain = jnp.where(image, gain_ref[1:2, columns], gain_ref[0:1, columns])
        staged[h] = (att[h].astype(jnp.float32) * inverse * gain).astype(staged.dtype)
        copy = pltpu.make_async_copy(
            staged.at[h], out_hbm.at[:, pl.ds(h * HEAD_DIM, HEAD_DIM)], out_sem.at[h]
        )
        copy.start()
        copies.append(copy)
    for copy in copies:
        copy.wait()


def on_device(n, queries, keys, values, segment_ids, modality, norm_gain):
    rows, width = queries.shape
    heads = width // HEAD_DIM
    vmem = pl.BlockSpec(memory_space=pltpu.VMEM)
    hbm = pl.BlockSpec(memory_space=pltpu.HBM)
    depth = 2 * rows // PIECES
    block = pltpu.VMEM((heads, PIECES, depth, HEAD_DIM), jnp.bfloat16)
    flow = pltpu.SemaphoreType.DMA((heads, PIECES))
    att, inverse, image = pl.pallas_call(
        functools.partial(kernel, n, heads, rows),
        out_shape=(
            pltpu.VMEM((heads, rows, HEAD_DIM), jnp.bfloat16),
            pltpu.VMEM((rows, HEAD_DIM), jnp.float32),
            pltpu.VMEM((rows, HEAD_DIM), jnp.int32),
        ),
        in_specs=[hbm, hbm, hbm, vmem, vmem],
        out_specs=(vmem, vmem, vmem),
        scratch_shapes=[
            pltpu.VMEM((heads, rows, HEAD_DIM), jnp.bfloat16),
            block,
            block,
            block,
            pltpu.VMEM((1, rows), jnp.int32),
            pltpu.VMEM((1, rows), jnp.int32),
            pltpu.VMEM((rows, (REACH + 1) * rows), jnp.float32),
            pltpu.VMEM((rows, HEAD_DIM), jnp.float32),
            pltpu.VMEM((rows, HEAD_DIM), jnp.float32),
            pltpu.VMEM((rows, HEAD_DIM), jnp.float32),
            pltpu.SemaphoreType.DMA((heads, PIECES + 1)),
            flow,
            flow,
            flow,
            flow,
            flow,
            pltpu.SemaphoreType.DMA((3,)),
            pltpu.SemaphoreType.DMA((2,)),
            pltpu.SemaphoreType.DMA((2,)),
        ],
        compiler_params=pltpu.CompilerParams(
            collective_id=0, has_side_effects=True
        ),
    )(queries, keys, values, segment_ids.reshape(1, rows), modality.reshape(1, rows))
    return pl.pallas_call(
        functools.partial(blend, heads),
        out_shape=jax.ShapeDtypeStruct((rows, width), jnp.bfloat16),
        in_specs=[vmem, vmem, vmem, vmem],
        out_specs=hbm,
        scratch_shapes=[
            pltpu.VMEM((heads, rows, HEAD_DIM), jnp.bfloat16),
            pltpu.SemaphoreType.DMA((heads,)),
        ],
        compiler_params=pltpu.CompilerParams(vmem_limit_bytes=8 * 2**20),
    )(att, inverse, image, norm_gain)


def solution(mesh):
    return jax.shard_map(
        functools.partial(on_device, mesh.shape["seq"]),
        mesh=mesh,
        in_specs=(
            P(("grp", "seq"), "tp"),
            P(("grp", "seq"), "tp"),
            P(("grp", "seq"), "tp"),
            P(("grp", "seq")),
            P(("grp", "seq")),
            P(None, "tp"),
        ),
        out_specs=P(("grp", "seq"), "tp"),
        check_vma=False,
    )
```

time: 37.3 us -> 34.3 us (0.920)
  local copies, waits for them, and re-layouts: 1.87 us -> 0.01 us
  Pallas kernels: 35.2 us -> 34.1 us
    unnamed x1 -> x2, local copies, waits for them, and re-layouts: 1.87 us -> 0.01 us
    pallas_call x1 -> x2, Pallas kernels: 35.2 us -> 34.1 us  [the longest x1 33.2 us: on_device(): pl.pallas_call(functools.partial(kernel, n, heads, rows), out_shape=(pltp...]
where the time goes in v2:
time: 34.3 us; the launch traced here: 34.1 us
  Pallas kernels  34.1 us (99%)
    pallas_call x1, Pallas kernels, on_device(): pl.pallas_call(functools.partial(kernel, n, heads, rows), out_shape=(pltp...  33.2 us
    pallas_call x1, Pallas kernels, on_device(): pl.pallas_call(functools.partial(blend, heads), out_shape=jax.ShapeDtypeS...  0.88 us

profile of v2, /device:TPU:17, one launch (start us, length us, event | category | flops | bytes accessed | tf_op | source)
XLA Modules:
  0.0 34.1 jit_solution(9722192724632738837)
XLA Ops:
  0.0 0.0 copy-start
  0.0 33.2 %shard_map.64 = (bf16[8,256,128]{2,1,0:T(8,128)(2,1)S(1)}, f32[256,128]{1,0:T(8,128)S(1)}, s32[256,128]{1,0:T(8,128)S(1)}) custom-call(bf16[256,1024]{1,0:T(8,128)(2,1)} %q_hbm.1, bf16[256,1024]{1,0:T(8,128)(2,1)} %k_hbm.1, bf16[256,1024]{1,0:T(8,128)(2,1)} %v_hbm.1, s32[1,256]{1,0:T(1,128)} %bitcast.2, s32[1,256]{1,0:T(1,128)} %bitcast.3), custom_call_target="tpu_custom_call" | custom-call | tf_op jit(solution)/shard_map/pallas_call | solution.py:311
  33.2 0.0 copy-done
  33.2 0.9 %shard_map.65 = bf16[256,1024]{1,0:T(8,128)(2,1)} custom-call(bf16[8,256,128]{2,1,0:T(8,128)(2,1)S(1)} %get-tuple-element.8.att, f32[256,128]{1,0:T(8,128)S(1)} %get-tuple-element.9.inverse_ref, s32[256,128]{1,0:T(8,128)S(1)} %get-tuple-element.10.image_ref, f32[2,1024]{1,0:T(2,128)S(1)} %copy-done), custom_call_target="tpu_custom_call" | custom-call | tf_op jit(solution)/shard_map/pallas_call | solution.py:345
Async XLA Ops:
  0.0 33.2 %copy-start = (f32[2,1024]{1,0:T(2,128)S(1)}, f32[2,1024]{1,0:T(2,128)}, u32[]{:S(2)}) copy-start(f32[2,1024]{1,0:T(2,128)} %gain_ref.1) | copy-start | bytes 24580

commit v3 on v2

--- a/solution.py
+++ b/solution.py
@@ -12,6 +12,7 @@
 REACH = 2
 MESH = pl.DeviceIdType.MESH
 PIECES = 4
+DIRECT = 2
 
 
 def kernel(
@@ -70,9 +71,14 @@
     def load_q(h):
         return pltpu.make_async_copy(q_hbm.at[:, columns_of(h)], q_own.at[h], in_sem.at[h, PIECES])
 
+    last = heads - 1
+    direct = range(PIECES - DIRECT, PIECES)
+    for p in direct:
+        load_piece(last, p).start()
     for h in range(heads):
         for p in range(PIECES):
-            load_piece(h, p).start()
+            if h < last or p not in direct:
+                load_piece(h, p).start()
 
     barrier = pltpu.get_barrier_semaphore()
     pl.semaphore_signal(barrier, inc=1, device_id={"tp": 1 - t}, device_id_type=MESH)
@@ -86,7 +92,18 @@
     def _():
         pl.semaphore_signal(barrier, inc=1, device_id={"seq": s - 2}, device_id_type=MESH)
 
-    peers = 2 + jnp.where(has_next, 1, 0) + jnp.where(has_prev, 1, 0)
+    ahead = odd & (s + 1 < n)
+    behind = even & has_prev
+
+    @pl.when(ahead)
+    def _():
+        pl.semaphore_signal(barrier, inc=1, device_id={"seq": s + 1}, device_id_type=MESH)
+
+    @pl.when(behind)
+    def _():
+        pl.semaphore_signal(barrier, inc=1, device_id={"seq": s - 1}, device_id_type=MESH)
+
+    peers = jnp.where(ahead, 1, 0) + jnp.where(behind, 1, 0) + 2 + jnp.where(has_next, 1, 0) + jnp.where(has_prev, 1, 0)
     pl.semaphore_wait(barrier, peers)
 
     def remote(source, target, send, recv, where):
@@ -108,6 +125,14 @@
     def flow_c(h, p):
         return remote(buf2.at[h, p], buf1.at[h, p], send_c.at[h, p], recv_1.at[h, p], pair)
 
+    def flow_d(p):
+        return remote(
+            own.at[last, p], buf1.at[last, p], send_c.at[last, p], recv_1.at[last, p], s + 1
+        )
+
+    def forwards(h, p):
+        return odd & has_prev & (h < last) if p in direct else odd & has_prev
+
     def seg_a():
         return remote(seg_ref, seg1, seg_send.at[0], seg_recv.at[0], pair)
 
@@ -125,22 +150,34 @@
     def _():
         seg_b().start()
 
+    for p in direct:
+        load_piece(last, p).wait()
+
+        @pl.when(ahead)
+        def _():
+            flow_d(p).start()
+
+    def send_pieces(h, waits):
+        for p in range(PIECES):
+            if p in waits:
+                load_piece(h, p).wait()
+
+            @pl.when(has_next)
+            def _():
+                flow_b(h, p).start()
+
+            @pl.when(even)
+            def _():
+                flow_a(h, p).start()
+
+        load_q(h).start()
+
     def send(h, carry):
-        for p in range(PIECES):
-            load_piece(h, p).wait()
-
-            @pl.when(has_next)
-            def _():
-                flow_b(h, p).start()
-
-            @pl.when(even)
-            def _():
-                flow_a(h, p).start()
-
-        load_q(h).start()
+        send_pieces(h, range(PIECES))
         return carry
 
-    lax.fori_loop(0, heads, send, 0)
+    lax.fori_loop(0, last, send, 0)
+    send_pieces(last, range(PIECES - DIRECT))
 
     @pl.when(s < 1)
     def _():
@@ -205,15 +242,24 @@
                 weight.astype(jnp.bfloat16), value, preferred_element_type=jnp.float32
             )
 
-        for p in range(PIECES):
+        for p in range(half):
 
             @pl.when(has_prev)
             def _():
                 flow_b(h, p).wait_recv()
 
-            @pl.when(odd & has_prev)
+            @pl.when(forwards(h, p))
             def _():
                 flow_c(h, p).start()
+
+        @pl.when(odd & has_prev)
+        def _():
+            for p in range(half, PIECES):
+                flow_b(h, p).wait_recv()
+
+                @pl.when(forwards(h, p))
+                def _():
+                    flow_c(h, p).start()
 
         near = scores_with(own, 0)
         far = scores_with(buf2, 2)
@@ -224,9 +270,15 @@
         far = jnp.exp(far - top)
         middle = jnp.exp(middle - top)
         total = jnp.sum(near + middle + far, axis=1, keepdims=True)
-        acc = product(near, own) + product(far, buf2)
+        acc = product(near, own)
+
+        @pl.when(behind)
+        def _():
+            for p in range(half, PIECES):
+                flow_b(h, p).wait_recv()
+
         arrive(h, range(half, PIECES))
-        acc = acc + product(middle, buf1)
+        acc = acc + product(far, buf2) + product(middle, buf1)
         attended = (acc * (1.0 / total)).astype(jnp.bfloat16)
         att[h] = attended
         wide = attended.astype(jnp.float32)
@@ -251,6 +303,12 @@
     inverse_ref[...] = lax.rsqrt(mean_square + 1e-05)
     swap.wait_send()
 
+    for p in direct:
+
+        @pl.when(ahead)
+        def _():
+            flow_d(p).wait_send()
+
     @pl.when(even)
     def _():
         seg_a().wait_send()
@@ -274,7 +332,7 @@
             def _():
                 flow_b(h, p).wait_send()
 
-            @pl.when(odd & has_prev)
+            @pl.when(forwards(h, p))
             def _():
                 flow_c(h, p).wait_send()
 

time: 34.3 us -> 35.6 us (1.038)
  Pallas kernels: 34.1 us -> 35.4 us
    pallas_call x1, Pallas kernels: 33.2 us -> 34.5 us  [on_device(): pl.pallas_call(functools.partial(kernel, n, heads, rows), out_shape=(pltp...]
where the time goes in v3:
time: 35.6 us; the launch traced here: 35.4 us
  Pallas kernels  35.4 us (99%)
    pallas_call x1, Pallas kernels, on_device(): pl.pallas_call(functools.partial(kernel, n, heads, rows), out_shape=(pltp...  34.5 us
    pallas_call x1, Pallas kernels, on_device(): pl.pallas_call(functools.partial(blend, heads), out_shape=jax.ShapeDtypeS...  0.88 us

profile of v3, /device:TPU:17, one launch (start us, length us, event | category | flops | bytes accessed | tf_op | source)
XLA Modules:
  0.0 35.4 jit_solution(16776253763843489175)
XLA Ops:
  0.0 0.0 copy-start
  0.0 34.5 %shard_map.64 = (bf16[8,256,128]{2,1,0:T(8,128)(2,1)S(1)}, f32[256,128]{1,0:T(8,128)S(1)}, s32[256,128]{1,0:T(8,128)S(1)}) custom-call(bf16[256,1024]{1,0:T(8,128)(2,1)} %q_hbm.1, bf16[256,1024]{1,0:T(8,128)(2,1)} %k_hbm.1, bf16[256,1024]{1,0:T(8,128)(2,1)} %v_hbm.1, s32[1,256]{1,0:T(1,128)} %bitcast.2, s32[1,256]{1,0:T(1,128)} %bitcast.3), custom_call_target="tpu_custom_call" | custom-call | tf_op jit(solution)/shard_map/pallas_call | solution.py:369
  34.5 0.0 copy-done
  34.5 0.9 %shard_map.65 = bf16[256,1024]{1,0:T(8,128)(2,1)} custom-call(bf16[8,256,128]{2,1,0:T(8,128)(2,1)S(1)} %get-tuple-element.8.att, f32[256,128]{1,0:T(8,128)S(1)} %get-tuple-element.9.inverse_ref, s32[256,128]{1,0:T(8,128)S(1)} %get-tuple-element.10.image_ref, f32[2,1024]{1,0:T(2,128)S(1)} %copy-done), custom_call_target="tpu_custom_call" | custom-call | tf_op jit(solution)/shard_map/pallas_call | solution.py:403
Async XLA Ops:
  0.0 34.5 %copy-start = (f32[2,1024]{1,0:T(2,128)S(1)}, f32[2,1024]{1,0:T(2,128)}, u32[]{:S(2)}) copy-start(f32[2,1024]{1,0:T(2,128)} %gain_ref.1) | copy-start | bytes 24580

commit v4 on v3

--- a/solution.py
+++ b/solution.py
@@ -31,6 +31,7 @@
     own,
     buf1,
     buf2,
+    hop,
     seg1,
     seg2,
     bias,
@@ -43,6 +44,7 @@
     send_c,
     recv_1,
     recv_2,
+    hop_recv,
     seg_send,
     seg_recv,
     sq_sem,
@@ -53,6 +55,9 @@
     odd = lax.rem(s, 2) == 1
     has_next = s + 2 < n
     has_prev = s >= 2
+    ahead = odd & (s + 1 < n)
+    passes = even & has_next
+    behind = even & has_prev
     pair = s + 1 - 2 * lax.rem(s, 2)
 
     half = PIECES // 2
@@ -92,18 +97,7 @@
     def _():
         pl.semaphore_signal(barrier, inc=1, device_id={"seq": s - 2}, device_id_type=MESH)
 
-    ahead = odd & (s + 1 < n)
-    behind = even & has_prev
-
-    @pl.when(ahead)
-    def _():
-        pl.semaphore_signal(barrier, inc=1, device_id={"seq": s + 1}, device_id_type=MESH)
-
-    @pl.when(behind)
-    def _():
-        pl.semaphore_signal(barrier, inc=1, device_id={"seq": s - 1}, device_id_type=MESH)
-
-    peers = jnp.where(ahead, 1, 0) + jnp.where(behind, 1, 0) + 2 + jnp.where(has_next, 1, 0) + jnp.where(has_prev, 1, 0)
+    peers = 2 + jnp.where(has_next, 1, 0) + jnp.where(has_prev, 1, 0)
     pl.semaphore_wait(barrier, peers)
 
     def remote(source, target, send, recv, where):
@@ -126,9 +120,12 @@
         return remote(buf2.at[h, p], buf1.at[h, p], send_c.at[h, p], recv_1.at[h, p], pair)
 
     def flow_d(p):
-        return remote(
-            own.at[last, p], buf1.at[last, p], send_c.at[last, p], recv_1.at[last, p], s + 1
-        )
+        i = p - direct[0]
+        return remote(own.at[last, p], hop.at[i], send_c.at[last, p], hop_recv.at[i], pair)
+
+    def flow_e(p):
+        i = p - direct[0]
+        return remote(hop.at[i], buf1.at[last, p], send_c.at[last, p], recv_1.at[last, p], s + 2)
 
     def forwards(h, p):
         return odd & has_prev & (h < last) if p in direct else odd & has_prev
@@ -214,6 +211,13 @@
 
     bias[:, rows : 2 * rows] = jnp.where(query_seg == seg1[...], 0.0, -jnp.inf)
     bias[:, 2 * rows :] = jnp.where(query_seg == seg2[...], 0.0, -jnp.inf)
+
+    for p in direct:
+
+        @pl.when(passes)
+        def _():
+            flow_d(p).wait_recv()
+            flow_e(p).start()
 
     def scores_of(query, key):
         return lax.dot_general(
@@ -308,6 +312,10 @@
         @pl.when(ahead)
         def _():
             flow_d(p).wait_send()
+
+        @pl.when(passes)
+        def _():
+            flow_e(p).wait_send()
 
     @pl.when(even)
     def _():
@@ -380,6 +388,7 @@
             block,
             block,
             block,
+            pltpu.VMEM((DIRECT, depth, HEAD_DIM), jnp.bfloat16),
             pltpu.VMEM((1, rows), jnp.int32),
             pltpu.VMEM((1, rows), jnp.int32),
             pltpu.VMEM((rows, (REACH + 1) * rows), jnp.float32),
@@ -392,6 +401,7 @@
             flow,
             flow,
             flow,
+            pltpu.SemaphoreType.DMA((DIRECT,)),
             pltpu.SemaphoreType.DMA((3,)),
             pltpu.SemaphoreType.DMA((2,)),
             pltpu.SemaphoreType.DMA((2,)),

time: 35.6 us -> 34.2 us (0.961)
  Pallas kernels: 35.4 us -> 34 us
    pallas_call x1, Pallas kernels: 34.5 us -> 33.1 us  [on_device(): pl.pallas_call(functools.partial(kernel, n, heads, rows), out_shape=(pltp...]
where the time goes in v4:
time: 34.2 us; the launch traced here: 34 us
  Pallas kernels  34 us (99%)
    pallas_call x1, Pallas kernels, on_device(): pl.pallas_call(functools.partial(kernel, n, heads, rows), out_shape=(pltp...  33.1 us
    pallas_call x1, Pallas kernels, on_device(): pl.pallas_call(functools.partial(blend, heads), out_shape=jax.ShapeDtypeS...  0.88 us

profile of v4, /device:TPU:17, one launch (start us, length us, event | category | flops | bytes accessed | tf_op | source)
XLA Modules:
  0.0 34.0 jit_solution(9111891491565109210)
XLA Ops:
  0.0 0.0 copy-start
  0.0 33.1 %shard_map.64 = (bf16[8,256,128]{2,1,0:T(8,128)(2,1)S(1)}, f32[256,128]{1,0:T(8,128)S(1)}, s32[256,128]{1,0:T(8,128)S(1)}) custom-call(bf16[256,1024]{1,0:T(8,128)(2,1)} %q_hbm.1, bf16[256,1024]{1,0:T(8,128)(2,1)} %k_hbm.1, bf16[256,1024]{1,0:T(8,128)(2,1)} %v_hbm.1, s32[1,256]{1,0:T(1,128)} %bitcast.2, s32[1,256]{1,0:T(1,128)} %bitcast.3), custom_call_target="tpu_custom_call" | custom-call | tf_op jit(solution)/shard_map/pallas_call | solution.py:377
  33.1 0.0 copy-done
  33.1 0.9 %shard_map.65 = bf16[256,1024]{1,0:T(8,128)(2,1)} custom-call(bf16[8,256,128]{2,1,0:T(8,128)(2,1)S(1)} %get-tuple-element.8.att, f32[256,128]{1,0:T(8,128)S(1)} %get-tuple-element.9.inverse_ref, s32[256,128]{1,0:T(8,128)S(1)} %get-tuple-element.10.image_ref, f32[2,1024]{1,0:T(2,128)S(1)} %copy-done), custom_call_target="tpu_custom_call" | custom-call | tf_op jit(solution)/shard_map/pallas_call | solution.py:413
Async XLA Ops:
  0.0 33.1 %copy-start = (f32[2,1024]{1,0:T(2,128)S(1)}, f32[2,1024]{1,0:T(2,128)}, u32[]{:S(2)}) copy-start(f32[2,1024]{1,0:T(2,128)} %gain_ref.1) | copy-start | bytes 24580

commit v5 on v4

--- a/solution.py
+++ b/solution.py
@@ -231,6 +231,23 @@
             def _():
                 flow_a(h, p).wait_recv()
 
+    def relay(h, p):
+        flow_b(h, p).wait_recv()
+
+        @pl.when(forwards(h, p))
+        def _():
+            flow_c(h, p).start()
+
+    def relay_next(h, p):
+        @pl.when(odd & has_prev & (h < last))
+        def _():
+            relay(h + 1, p)
+
+    @pl.when(odd & has_prev)
+    def _():
+        for p in range(PIECES):
+            relay(0, p)
+
     def head(h, carry):
         load_q(h).wait()
         query = q_own[h]
@@ -246,34 +263,23 @@
                 weight.astype(jnp.bfloat16), value, preferred_element_type=jnp.float32
             )
 
-        for p in range(half):
-
-            @pl.when(has_prev)
-            def _():
+        @pl.when(behind)
+        def _():
+            for p in range(half):
                 flow_b(h, p).wait_recv()
 
-            @pl.when(forwards(h, p))
-            def _():
-                flow_c(h, p).start()
-
-        @pl.when(odd & has_prev)
-        def _():
-            for p in range(half, PIECES):
-                flow_b(h, p).wait_recv()
-
-                @pl.when(forwards(h, p))
-                def _():
-                    flow_c(h, p).start()
-
+        relay_next(h, 0)
         near = scores_with(own, 0)
         far = scores_with(buf2, 2)
         arrive(h, range(half))
         middle = scores_with(buf1, 1)
+        relay_next(h, 1)
         top = jnp.max(jnp.maximum(jnp.maximum(near, middle), far), axis=1, keepdims=True)
         near = jnp.exp(near - top)
         far = jnp.exp(far - top)
         middle = jnp.exp(middle - top)
         total = jnp.sum(near + middle + far, axis=1, keepdims=True)
+        relay_next(h, 2)
         acc = product(near, own)
 
         @pl.when(behind)
@@ -283,6 +289,7 @@
 
         arrive(h, range(half, PIECES))
         acc = acc + product(far, buf2) + product(middle, buf1)
+        relay_next(h, 3)
         attended = (acc * (1.0 / total)).astype(jnp.bfloat16)
         att[h] = attended
         wide = attended.astype(jnp.float32)

time: 34.2 us -> 34.2 us (level)
  no operation moved by 1% of the time
where the time goes in v5:
time: 34.2 us; the launch traced here: 34 us
  Pallas kernels  34 us (99%)
    pallas_call x1, Pallas kernels, on_device(): pl.pallas_call(functools.partial(kernel, n, heads, rows), out_shape=(pltp...  33.1 us
    pallas_call x1, Pallas kernels, on_device(): pl.pallas_call(functools.partial(blend, heads), out_shape=jax.ShapeDtypeS...  0.88 us

profile of v5, /device:TPU:17, one launch (start us, length us, event | category | flops | bytes accessed | tf_op | source)
XLA Modules:
  0.0 34.0 jit_solution(2566287012839056830)
XLA Ops:
  0.0 0.0 copy-start
  0.0 33.1 %shard_map.64 = (bf16[8,256,128]{2,1,0:T(8,128)(2,1)S(1)}, f32[256,128]{1,0:T(8,128)S(1)}, s32[256,128]{1,0:T(8,128)S(1)}) custom-call(bf16[256,1024]{1,0:T(8,128)(2,1)} %q_hbm.1, bf16[256,1024]{1,0:T(8,128)(2,1)} %k_hbm.1, bf16[256,1024]{1,0:T(8,128)(2,1)} %v_hbm.1, s32[1,256]{1,0:T(1,128)} %bitcast.2, s32[1,256]{1,0:T(1,128)} %bitcast.3), custom_call_target="tpu_custom_call" | custom-call | tf_op jit(solution)/shard_map/pallas_call | solution.py:384
  33.1 0.0 copy-done
  33.2 0.9 %shard_map.65 = bf16[256,1024]{1,0:T(8,128)(2,1)} custom-call(bf16[8,256,128]{2,1,0:T(8,128)(2,1)S(1)} %get-tuple-element.8.att, f32[256,128]{1,0:T(8,128)S(1)} %get-tuple-element.9.inverse_ref, s32[256,128]{1,0:T(8,128)S(1)} %get-tuple-element.10.image_ref, f32[2,1024]{1,0:T(2,128)S(1)} %copy-done), custom_call_target="tpu_custom_call" | custom-call | tf_op jit(solution)/shard_map/pallas_call | solution.py:420
Async XLA Ops:
  0.0 33.1 %copy-start = (f32[2,1024]{1,0:T(2,128)S(1)}, f32[2,1024]{1,0:T(2,128)}, u32[]{:S(2)}) copy-start(f32[2,1024]{1,0:T(2,128)} %gain_ref.1) | copy-start | bytes 24580

commit v6 on v5

--- a/solution.py
+++ b/solution.py
@@ -12,7 +12,7 @@
 REACH = 2
 MESH = pl.DeviceIdType.MESH
 PIECES = 4
-DIRECT = 2
+DIRECT = 1
 
 
 def kernel(

time: 34.2 us -> 34.2 us (level)
  no operation moved by 1% of the time
where the time goes in v6:
time: 34.2 us; the launch traced here: 34 us
  Pallas kernels  34 us (99%)
    pallas_call x1, Pallas kernels, on_device(): pl.pallas_call(functools.partial(kernel, n, heads, rows), out_shape=(pltp...  33.1 us
    pallas_call x1, Pallas kernels, on_device(): pl.pallas_call(functools.partial(blend, heads), out_shape=jax.ShapeDtypeS...  0.88 us

profile of v6, /device:TPU:17, one launch (start us, length us, event | category | flops | bytes accessed | tf_op | source)
XLA Modules:
  0.0 34.0 jit_solution(7339480095714252173)
XLA Ops:
  0.0 0.0 copy-start
  0.0 33.1 %shard_map.64 = (bf16[8,256,128]{2,1,0:T(8,128)(2,1)S(1)}, f32[256,128]{1,0:T(8,128)S(1)}, s32[256,128]{1,0:T(8,128)S(1)}) custom-call(bf16[256,1024]{1,0:T(8,128)(2,1)} %q_hbm.1, bf16[256,1024]{1,0:T(8,128)(2,1)} %k_hbm.1, bf16[256,1024]{1,0:T(8,128)(2,1)} %v_hbm.1, s32[1,256]{1,0:T(1,128)} %bitcast.2, s32[1,256]{1,0:T(1,128)} %bitcast.3), custom_call_target="tpu_custom_call" | custom-call | tf_op jit(solution)/shard_map/pallas_call | solution.py:384
  33.1 0.0 copy-done
  33.1 0.9 %shard_map.65 = bf16[256,1024]{1,0:T(8,128)(2,1)} custom-call(bf16[8,256,128]{2,1,0:T(8,128)(2,1)S(1)} %get-tuple-element.8.att, f32[256,128]{1,0:T(8,128)S(1)} %get-tuple-element.9.inverse_ref, s32[256,128]{1,0:T(8,128)S(1)} %get-tuple-element.10.image_ref, f32[2,1024]{1,0:T(2,128)S(1)} %copy-done), custom_call_target="tpu_custom_call" | custom-call | tf_op jit(solution)/shard_map/pallas_call | solution.py:420
Async XLA Ops:
  0.0 33.1 %copy-start = (f32[2,1024]{1,0:T(2,128)S(1)}, f32[2,1024]{1,0:T(2,128)}, u32[]{:S(2)}) copy-start(f32[2,1024]{1,0:T(2,128)} %gain_ref.1) | copy-start | bytes 24580
